TPU v7x, 256 devices: a 2x2x32 block of a 4x8x32 slice. The times are simulated.
256 devices in a mesh: groups: 4 (over y, x), rows: 64 (over z, core).
Axes of the slice: x: 2, y: 2, z: 32, core: 2. Of those that a mesh axis runs over, the one named last changes fastest.
The devices are a block of a 4x8x32 slice.
Arguments:
- queries: bfloat16 [4096, 8192], P(('groups', 'rows')), parts along dimension 0, may hold values from -6 to 6
- sketches: bfloat16 [131072, 8192], P(('groups', 'rows')), parts along dimension 0, may hold values from -16 to 16, as said below
- row_ids: int32 [131072], P(('groups', 'rows')), parts along dimension 0, may hold values from 0 to 32767, each once
Outputs:
- top_scores: float32 [4096, 128], P(('groups', 'rows')), parts along dimension 0
There are 4 independent parts, one for each index of `groups`. A program takes and returns all parts, laid end to end along the dimension named above; each array names one. Nothing has to cross between parts.
Inputs may be any that keep to these rules, and one draw needn't show every extreme that they name: `sketches`: sketch entries are real-valued.
All inputs are finite; a program needn't handle non-finite values.
Results may differ from a plain program's by a relative error of at most 0.0003.
Values may be sent and summed in bfloat16 or wider, within the bound.
A program may use at most 128 MiB of HBM per device.

v0:
```python
import jax
import jax.numpy as jnp
from jax import lax
from jax.sharding import PartitionSpec as P

TOPK = 128


def split_up(value, dim, length):
    shape = value.shape
    blocks = value.reshape(*shape[:dim], length, shape[dim] // length, *shape[dim + 1 :])
    return jnp.moveaxis(blocks, dim, 0)


def summed_on_arrival(value, axis, dim):
    length = lax.axis_size(axis)
    blocks = lax.all_to_all(split_up(value, dim, length), axis, 0, 0, tiled=True)
    return jnp.sum(blocks, axis=0)


def shards(queries, sketches, row_ids):
    devices = lax.axis_size("rows")
    total_rows = sketches.shape[0] * devices
    retired = total_rows // 4
    live_count = total_rows - retired
    keep = TOPK
    scores = lax.dot_general(
        lax.all_gather(queries, "rows", axis=0, tiled=True),
        sketches,
        (((1,), (1,)), ((), ())),
        preferred_element_type=jnp.float32,
    )
    live = row_ids >= retired
    square_sum = jnp.sum(jnp.where(live[None, :], scores * scores, jnp.float32(0.0)), axis=1)
    masked = jnp.where(live[None, :], scores, jnp.float32(-1e30))
    candidates = lax.top_k(masked, keep)[0]
    payload = (candidates,)
    own_sum = summed_on_arrival(square_sum, "rows", 0)
    received = (lax.all_to_all(payload[0], "rows", split_axis=0, concat_axis=1, tiled=True),)
    best = lax.top_k(received[0], keep)[0]
    inverse_scale = lax.rsqrt(own_sum / jnp.float32(live_count) + jnp.float32(1e-06))
    return best * inverse_scale[:, None]


def solution(mesh):
    return jax.shard_map(
        shards,
        mesh=mesh,
        in_specs=(P(("groups", "rows"), None), P(("groups", "rows"), None), P(("groups", "rows"))),
        out_specs=P(("groups", "rows"), None),
        check_vma=False,
    )
```

profile of v0, /device:TPU:37, one launch (start us, length us, event | category | flops | bytes accessed | tf_op | source)
XLA Modules:
  0.0 373.6 jit_solution(11457842833696534099)
XLA Ops:
  6.5 0.0 all-gather.2.cloned.1.call-start
  6.6 0.7 all-gather.2.cloned.1.call-update
  7.3 0.7 broadcast_compare_fusion
  8.0 162.5 %all-gather.2.cloned.1.call-done = bf16[1024,8192]{1,0:T(8,128)(2,1)} async-done(((bf16[16,8192]{1,0:T(8,128)(2,1)}), bf16[1024,8192]{1,0:T(8,128)(2,1)}) %all-gather.2.cloned.1.call-update) | async-done | bytes 16777232 | tf_op jit(solution)/shard_map/all_gather | solution.py:28
  170.5 15.9 %select_reduce_fusion = (f32[1024]{0:T(1024)S(1)}, f32[1024,512]{0,1:T(8,128)}) fusion(pred[512]{0:T(512)(128)(4,1)S(1)} %broadcast_compare_fusion, bf16[1024,8192]{1,0:T(8,128)(2,1)} %all-gather.2.cloned.1.call-done, bf16[512,8192]{1,0:T(8,128)(2,1)} %param.4), kind=kOutput, calls=%fused_computation | convolution fusion | flops 8592030720 | bytes 27267584 | tf_op jit(solution)/shard_map/dot_general | solution.py:27
  186.3 0.7 all_to_all.24
  187.0 13.5 %all-to-all-start.1 = ((f32[64,1,16]{2,1,0:T(1,128)}), f32[64,1,16]{2,1,0:T(1,128)S(1)}, u32[]{:S(2)}, u32[]{:S(2)}) async-start(f32[64,1,16]{2,1,0:T(1,128)} %bitcast.2), calls=%async_computation.1 | async-start | bytes 65536 | tf_op jit(solution)/shard_map/all_to_all | solution.py:17
  200.5 0.1 iota.6.clone
  200.7 58.5 %top_k.14 = (f32[1024,512]{0,1:T(8,128)}, s32[1024,512]{0,1:T(8,128)}) sort(f32[1024,512]{0,1:T(8,128)} %get-tuple-element.15, s32[1024,512]{0,1:T(8,128)S(1)} %iota.6.clone), dimensions={1}, to_apply=%region_0.1 | sort | flops 9961472 | bytes 8388608 | tf_op jit(solution)/shard_map/top_k | solution.py:36
  259.2 1.9 copy.11
  261.1 0.9 top_k.22
  262.0 0.0 all-to-all-done.1
  262.0 23.2 %all-to-all-start = ((f32[64,16,128]{2,1,0:T(8,128)}), f32[64,16,128]{2,1,0:T(8,128)S(1)}, u32[]{:S(2)}, u32[]{:S(2)}) async-start(f32[64,16,128]{2,1,0:T(8,128)} %bitcast), calls=%async_computation | async-start | bytes 1048576 | tf_op jit(solution)/shard_map/all_to_all | solution.py:39
  285.2 0.1 reduce_sum.19
  285.3 63.9 %all-to-all-done = f32[64,16,128]{2,1,0:T(8,128)S(1)} async-done(((f32[64,16,128]{2,1,0:T(8,128)}), f32[64,16,128]{2,1,0:T(8,128)S(1)}, u32[]{:S(2)}, u32[]{:S(2)}) %all-to-all-start) | async-done | bytes 524320 | tf_op jit(solution)/shard_map/all_to_all | solution.py:39
  349.2 16.8 %sort_prefixfusion = f32[16,128]{1,0:T(8,128)S(1)} fusion(f32[16,8192]{1,0:T(8,128)S(1)} %copy_bitcast_fusion), kind=kCustom, calls=%top_k.20.sort_prefix | custom fusion | flops 2228224 | bytes 532480 | tf_op jit(solution)/shard_map/top_k | solution.py:40
  366.0 0.7 broadcast_multiply_fusion
  (2 shorter events, 0.0 us)
Async XLA Ops:
  6.5 163.9 %all-gather.2.cloned.1.call-start = ((), (), s32[]{:S(2)}) async-start(), calls=%async_computation.2 | async-start | bytes 17039360 | tf_op jit(solution)/shard_map/all_gather | solution.py:28
  187.0 75.0 %all-to-all-start.1 = ((f32[64,1,16]{2,1,0:T(1,128)}), f32[64,1,16]{2,1,0:T(1,128)S(1)}, u32[]{:S(2)}, u32[]{:S(2)}) async-start(f32[64,1,16]{2,1,0:T(1,128)} %bitcast.2), calls=%async_computation.1 | async-start | bytes 65536 | tf_op jit(solution)/shard_map/all_to_all | solution.py:17
  262.0 87.2 %all-to-all-start = ((f32[64,16,128]{2,1,0:T(8,128)}), f32[64,16,128]{2,1,0:T(8,128)S(1)}, u32[]{:S(2)}, u32[]{:S(2)}) async-start(f32[64,16,128]{2,1,0:T(8,128)} %bitcast), calls=%async_computation | async-start | bytes 1048576 | tf_op jit(solution)/shard_map/all_to_all | solution.py:39
Sparse Core Ops, SparseCore 0:
  9.2 161.2 all-gather.1
where the time goes:
time: 374 us
  waiting for transfers between devices  227 us (61%)
  other arithmetic  76.8 us (21%)
  starting transfers between devices  36.8 us (10%)
  matrix products  15.9 us (4%)
  between operations  13.5 us (4%)
    all_gather x1, waiting for transfers between devices, shards(): lax.all_gather(queries, 'rows', axis=0, tiled=True)  163 us
    all_to_all x1, waiting for transfers between devices, shards(): lax.all_to_all(payload[0], 'rows', split_axis=0, concat_axis=1, tiled=True)  63.9 us
    top_k x1, other arithmetic, shards(): candidates = lax.top_k(masked, keep)[0]  58.5 us
    all_to_all x1, starting transfers between devices, shards(): lax.all_to_all(payload[0], 'rows', split_axis=0, concat_axis=1, tiled=True)  23.2 us
    top_k x1, other arithmetic, shards(): best = lax.top_k(received[0], keep)[0]  16.8 us
    dot_general x1, matrix products, shards(): lax.dot_general(lax.all_gather(queries, 'rows', axis=0, tiled=True), sket...  15.9 us
    all_to_all x1, starting transfers between devices, summed_on_arrival(): lax.all_to_all(split_up(value, dim, length), axis, 0, 0, tiled=True)  13.5 us
  transfers between devices with their start and end apart: 3, of which 2 were waited for; matrix products, arithmetic and copies ran while one was open for 17% of the time, Pallas kernels for 0%

commit v1 on v0

v1 whole, which is shorter than its diff:
```python
import functools

import jax
import jax.numpy as jnp
from jax import lax
from jax.experimental import pallas as pl
from jax.experimental.pallas import tpu as pltpu
from jax.sharding import PartitionSpec as P

TOPK = 128
LANES = 128
SUB = 8
CHUNKS = 8
DELAY = 3
DEAD = -1e30


def exchange(a, b):
    return jnp.maximum(a, b), jnp.minimum(a, b)


def sort_pairs(n):
    pairs = []

    def merge(lo, length, step):
        double = step * 2
        if double < length:
            merge(lo, length, double)
            merge(lo + step, length, double)
            for i in range(lo + step, lo + length - step, double):
                pairs.append((i, i + step))
        else:
            pairs.append((lo, lo + step))

    def sort(lo, length):
        if length > 1:
            half = length // 2
            sort(lo, half)
            sort(lo + half, half)
            merge(lo, length, 1)

    sort(0, n)
    return pairs


def descend(values, gap):
    values = list(values)
    while gap >= 1:
        for i in range(len(values)):
            if i % (2 * gap) < gap:
                values[i], values[i + gap] = exchange(values[i], values[i + gap])
        gap //= 2
    return values


class Rows:
    def __init__(self, ref, base=0):
        self.ref, self.base = ref, base

    def at(self, i):
        start = (self.base + i) * SUB
        if not isinstance(start, int):
            start = pl.multiple_of(start, SUB)
        return pl.ds(start, SUB)

    def load(self, i):
        return self.ref[self.at(i), :]

    def store(self, i, value):
        self.ref[self.at(i), :] = value


def finish(rows, count):
    for block in range(0, count, 16):
        values = descend([rows.load(block + i) for i in range(16)], 8)
        for i in range(16):
            rows.store(block + i, values[i])


def join(rows, size):
    half = size // 2
    firsts = range(0, half, 16)
    for i in range(16):
        index = [i + k for k in firsts] + [size - 1 - i - k for k in reversed(firsts)]
        low = len(firsts)
        values = [rows.load(k) for k in index]
        for k in range(low):
            values[k], values[2 * low - 1 - k] = exchange(values[k], values[2 * low - 1 - k])
        values = descend(values[:low], low // 2) + descend(values[low:], low // 2)
        for k, value in zip(index, values):
            rows.store(k, value)
    finish(rows, size)


def prune(left, right, out, keep, view=lambda value: value):
    for i in range(16):
        index = list(range(i, keep, 16))
        values = [jnp.maximum(left.load(k), view(right.load(keep - 1 - k))) for k in index]
        values = descend(values, len(index) // 2)
        for k, value in zip(index, values):
            out.store(k, value)
    finish(out, keep)


def sort_rows(ref, count, keep):
    network = sort_pairs(16)

    @pl.loop(0, count // 16)
    def _(block):
        rows = Rows(ref, block * 16)
        values = [rows.load(i) for i in range(16)]
        for a, b in network:
            values[a], values[b] = exchange(values[a], values[b])
        for i in range(16):
            rows.store(i, values[i])

    @pl.loop(0, count // 32)
    def _(block):
        rows = Rows(ref, block * 32)
        values = [rows.load(i) for i in range(32)]
        for i in range(16):
            values[i], values[31 - i] = exchange(values[i], values[31 - i])
        values = descend(values[:16], 8) + descend(values[16:], 8)
        for i in range(32):
            rows.store(i, values[i])

    size = 64
    while size <= keep:

        @pl.loop(0, count // size)
        def _(block, size=size):
            join(Rows(ref, block * size), size)

        size *= 2

    runs = count // keep
    gap = 1
    while gap < runs:

        @pl.loop(0, runs // (2 * gap))
        def _(pair, gap=gap):
            left = Rows(ref, pair * (2 * gap * keep))
            right = Rows(ref, pair * (2 * gap * keep) + gap * keep)
            prune(left, right, left, keep)

        gap *= 2


def kernel(
    chips, retired, live_count,
    queries, sketches, row_ids, out,
    gathered, rows, live, total, scores, square, lists, square_in, other, sent, received, square_received,
    load_sem, link_send, link_recv, die_send, die_recv, pair_send, pair_recv, list_send, list_recv, sum_send, sum_recv,
):
    count, width = rows.shape
    own = queries.shape[0]
    columns = width // CHUNKS
    per_batch = LANES // (2 * own)
    pieces = per_batch * CHUNKS
    depth = width // pieces
    batches = chips // per_batch
    me = lax.axis_index("rows")
    chip, core = me // 2, me % 2
    step = 1 - 2 * core
    following = {"rows": ((chip + chips + step) % chips) * 2 + core}
    previous = {"rows": ((chip + chips - step) % chips) * 2 + core}
    sibling = {"rows": chip * 2 + (1 - core)}
    mesh_id = pl.DeviceIdType.MESH

    def place(distance, stream):
        return pl.ds(pl.multiple_of((distance * 2 + stream) * own, own), own)

    def part(j):
        return pl.ds(pl.multiple_of(j * columns, LANES), columns)

    def over_link(distance, j):
        return pltpu.make_async_remote_copy(
            gathered.at[place(distance, core), part(j)],
            gathered.at[place(distance + 1, core), part(j)],
            link_send.at[distance % 2, j], link_recv.at[distance + 1, j],
            device_id=following, device_id_type=mesh_id,
        )

    def over_die(distance, j):
        return pltpu.make_async_remote_copy(
            gathered.at[place(distance, core), part(j)],
            gathered.at[place(distance, core), part(j)],
            die_send.at[distance % 2, j], die_recv.at[distance, j],
            device_id=sibling, device_id_type=mesh_id,
        )

    load_queries = pltpu.make_async_copy(queries, gathered.at[place(0, core), :], load_sem.at[0])
    load_queries.start()
    load_rows = pltpu.make_async_copy(sketches, rows, load_sem.at[1])
    load_rows.start()
    barrier = pltpu.get_barrier_semaphore()
    for device in (following, previous, sibling):
        pl.semaphore_signal(barrier, inc=1, device_id=device, device_id_type=mesh_id)

    for block in range(count // LANES):
        ids = row_ids[pl.ds(block, 1), :]
        flags = jnp.where(ids >= retired, jnp.float32(1.0), jnp.float32(0.0))
        live[pl.ds(block * LANES, LANES), :] = jnp.broadcast_to(flags, (LANES, LANES)).T
    load_queries.wait()
    pl.semaphore_wait(barrier, 3)

    def compute(piece):
        batch, k = piece // pieces, piece % pieces

        @pl.when(k == 0)
        def _():
            @pl.loop(0, pieces)
            def _(index):
                over_die(batch * per_batch + index // CHUNKS, index % CHUNKS).wait_recv()

            total[...] = jnp.zeros_like(total)

        cut = pl.ds(pl.multiple_of(k * depth, LANES), depth)
        total[...] += lax.dot_general(
            rows[:, cut],
            gathered[pl.ds(pl.multiple_of(batch * LANES, LANES), LANES), cut],
            (((1,), (1,)), ((), ())),
            preferred_element_type=jnp.float32,
        )

        @pl.when(k == pieces - 1)
        def _():
            kept = live[...] > 0.5
            value = total[...]
            squares = jnp.where(kept, value * value, jnp.float32(0.0))
            square[batch] = jnp.sum(squares, axis=0, keepdims=True)
            scores[pl.ds(batch, count, stride=SUB), :] = jnp.where(kept, value, jnp.float32(DEAD))

    first = per_batch * CHUNKS + DELAY

    @pl.loop(0, chips * CHUNKS)
    def _(slot):
        distance, j = slot // CHUNKS, slot % CHUNKS

        @pl.when(distance > 0)
        def _():
            over_link(distance - 1, j).wait_recv()

        @pl.when(distance < chips - 1)
        def _():
            @pl.when(distance >= 2)
            def _():
                over_link(distance - 2, j).wait_send()

            over_link(distance, j).start()

        @pl.when(distance >= 2)
        def _():
            over_die(distance - 2, j).wait_send()

        over_die(distance, j).start()

        @pl.when(slot == first)
        def _():
            load_rows.wait()

        @pl.when(slot >= first)
        def _():
            compute(slot - first)

    @pl.loop(chips * CHUNKS - first, batches * pieces)
    def _(piece):
        compute(piece)

    @pl.loop(0, 2 * CHUNKS)
    def _(index):
        over_link(chips - 3 + index // CHUNKS, index % CHUNKS).wait_send()
        over_die(chips - 2 + index // CHUNKS, index % CHUNKS).wait_send()

    sort_rows(scores, count, TOPK)

    @pl.loop(0, TOPK)
    def _(i):
        at = pl.ds(pl.multiple_of(i * SUB, SUB), SUB)
        lists[at, :] = scores[at, :]

    to_sibling = pltpu.make_async_remote_copy(
        lists, other, pair_send.at[0], pair_recv.at[0], device_id=sibling, device_id_type=mesh_id
    )
    to_sibling.start()
    sums_to_sibling = pltpu.make_async_remote_copy(
        square, square_in, pair_send.at[1], pair_recv.at[1], device_id=sibling, device_id_type=mesh_id
    )
    sums_to_sibling.start()
    to_sibling.wait()
    sums_to_sibling.wait()
    square_in[...] = square_in[...] + square[...]
    prune(Rows(lists), Rows(other), Rows(scores), TOPK)

    for batch in range(batches):
        sent[pl.ds(batch * LANES, LANES), :] = scores[pl.ds(batch, TOPK, stride=SUB), :].T

    def owner(distance):
        return {"rows": ((chip + chips - step * distance) % chips) * 2 + core}

    def list_out(distance):
        return pltpu.make_async_remote_copy(
            sent.at[place(distance, core), :],
            received.at[pl.ds(pl.multiple_of(distance * own, own), own), :],
            list_send.at[distance], list_recv.at[distance],
            device_id=owner(distance), device_id_type=mesh_id,
        )

    def sum_out(distance):
        return pltpu.make_async_remote_copy(
            square_in.at[distance // per_batch],
            square_received.at[distance],
            sum_send.at[distance], sum_recv.at[distance],
            device_id=owner(distance), device_id_type=mesh_id,
        )

    half = chips // 2

    @pl.loop(0, chips - 1)
    def _(index):
        near = half - (index + 1) // 2
        distance = jnp.where(index % 2 == 0, near, chips - near)
        list_out(distance).start()
        sum_out(distance).start()

    received[pl.ds(0, own), :] = sent[place(0, core), :]
    square_received[0] = square_in[0]

    @pl.loop(1, chips)
    def _(distance):
        list_out(distance).wait()
        sum_out(distance).wait()

    row = jnp.zeros((1, LANES), jnp.float32)
    for inside in range(per_batch):
        term = square_received[inside]
        for batch in range(1, batches):
            term = term + square_received[batch * per_batch + inside]
        shift = inside * 2 * own
        row = row + (pltpu.roll(term, LANES - shift, 1) if shift else term)
    row = jnp.where(core == 0, row, pltpu.roll(row, LANES - own, 1))
    squares = jnp.broadcast_to(row, (LANES, LANES)).T[:own, :]
    inverse = lax.rsqrt(squares / jnp.float32(live_count) + jnp.float32(1e-6))

    held = chips * own // LANES
    for block in range(held):
        scores[pl.ds(block, TOPK, stride=SUB), :] = received[pl.ds(block * LANES, LANES), :].T
    source, target = scores, lists
    views = []
    gap = held // 2
    while gap >= 1:
        views.append((0, SUB - gap))
        gap //= 2
    gap = LANES // 2
    while gap >= own:
        views.append((1, LANES - gap))
        gap //= 2
    for axis, shift in views:
        prune(
            Rows(source), Rows(source), Rows(target), TOPK,
            lambda value, axis=axis, shift=shift: pltpu.roll(value, shift, axis),
        )
        source, target = target, (scores if target is lists else lists)
    best = source[pl.ds(0, TOPK, stride=SUB), :].T[:own, :]
    out[...] = best * inverse


def shards(queries, sketches, row_ids):
    devices = lax.axis_size("rows")
    chips = devices // 2
    count, width = sketches.shape
    own = queries.shape[0]
    total_rows = count * devices
    retired = total_rows // 4
    per_batch = LANES // (2 * own)
    batches = chips // per_batch
    f32 = jnp.float32
    dma = pltpu.SemaphoreType.DMA
    return pl.pallas_call(
        functools.partial(kernel, chips, retired, total_rows - retired),
        out_shape=jax.ShapeDtypeStruct((own, TOPK), f32),
        in_specs=[
            pl.BlockSpec(memory_space=pl.ANY),
            pl.BlockSpec(memory_space=pl.ANY),
            pl.BlockSpec(memory_space=pltpu.VMEM),
        ],
        out_specs=pl.BlockSpec(memory_space=pltpu.VMEM),
        scratch_shapes=[
            pltpu.VMEM((devices * own, width), jnp.bfloat16),
            pltpu.VMEM((count, width), jnp.bfloat16),
            pltpu.VMEM((count, LANES), f32),
            pltpu.VMEM((count, LANES), f32),
            pltpu.VMEM((count * SUB, LANES), f32),
            pltpu.VMEM((batches, 1, LANES), f32),
            pltpu.VMEM((TOPK * SUB, LANES), f32),
            pltpu.VMEM((batches, 1, LANES), f32),
            pltpu.VMEM((TOPK * SUB, LANES), f32),
            pltpu.VMEM((devices * own, TOPK), f32),
            pltpu.VMEM((chips * own, TOPK), f32),
            pltpu.VMEM((chips, 1, LANES), f32),
            dma((2,)),
            dma((2, CHUNKS)), dma((chips, CHUNKS)),
            dma((2, CHUNKS)), dma((chips, CHUNKS)),
            dma((2,)), dma((2,)),
            dma((chips,)), dma((chips,)), dma((chips,)), dma((chips,)),
        ],
        compiler_params=pltpu.CompilerParams(
            collective_id=0, has_side_effects=True, vmem_limit_bytes=60 * 1024 * 1024
        ),
        name="attribute",
    )(queries, sketches, row_ids.reshape(count // LANES, LANES))


def solution(mesh):
    return jax.shard_map(
        shards,
        mesh=mesh,
        in_specs=(P(("groups", "rows"), None), P(("groups", "rows"), None), P(("groups", "rows"))),
        out_specs=P(("groups", "rows"), None),
        check_vma=False,
    )
```

time: 374 us -> 175 us (0.47)
  waiting for transfers between devices: 227 us -> 0 us
  Pallas kernels: 0 us -> 173 us
  other arithmetic: 76.8 us -> 0 us
  starting transfers between devices: 36.8 us -> 0 us
  matrix products: 15.9 us -> 0 us
  between operations: 13.5 us -> 0.01 us
    pallas_call x0 -> x1, Pallas kernels: none -> 173 us  [shards(): pl.pallas_call(functools.partial(kernel, chips, retired, total_rows - ret...]
    all_gather x1 -> x0, waiting for transfers between devices: 163 us -> none  [shards(): lax.all_gather(queries, 'rows', axis=0, tiled=True)]
    top_k x2 -> x0, other arithmetic: 75.3 us -> none  [the longest x1 58.5 us: shards(): candidates = lax.top_k(masked, keep)[0]]
    all_to_all x2 -> x0, waiting for transfers between devices: 63.9 us -> none  [the longest x1 63.9 us: shards(): lax.all_to_all(payload[0], 'rows', split_axis=0, concat_axis=1, tiled=True)]
    all_to_all x2 -> x0, starting transfers between devices: 36.8 us -> none  [the longest x1 23.2 us: shards(): lax.all_to_all(payload[0], 'rows', split_axis=0, concat_axis=1, tiled=True)]
    dot_general x1 -> x0, matrix products: 15.9 us -> none  [shards(): lax.dot_general(lax.all_gather(queries, 'rows', axis=0, tiled=True), sket...]
  transfers between devices with their start and end apart: 3 -> 0, of which waited for: 2 -> 0; matrix products, arithmetic and copies ran while one was open for 17% -> 0% of each run, Pallas kernels for 0% -> 0%
where the time goes in v1:
time: 175 us; the launch traced here: 174 us
  Pallas kernels  173 us (99%)
    pallas_call x1, Pallas kernels, shards(): pl.pallas_call(functools.partial(kernel, chips, retired, total_rows - ret...  173 us

profile of v1, /device:TPU:37, one launch (start us, length us, event | category | flops | bytes accessed | tf_op | source)
XLA Modules:
  0.0 174.2 jit_solution(8942059882993525942)
XLA Ops:
  0.0 172.9 %attribute.1 = f32[16,128]{1,0:T(8,128)} custom-call(bf16[16,8192]{1,0:T(8,128)(2,1)} %queries.1, bf16[512,8192]{1,0:T(8,128)(2,1)} %sketches.1, s32[4,128]{1,0:T(4,128)} %bitcast.1), custom_call_target="tpu_custom_call" | custom-call | tf_op jit(solution)/shard_map/attribute/pallas_call | solution.py:379
  172.9 1.3 copy.5
